TPU v7x, 32 devices: a whole 2x2x4 slice. The times are simulated.
32 devices in a mesh: clu: 16 (over z, y, x), col: 2 (over core).
Axes of the slice: x: 2, y: 2, z: 4, core: 2. Of those that a mesh axis runs over, the one named last changes fastest.
Arguments:
- features: bfloat16 [16384, 2048], P('clu', 'col'), may hold values from -6 to 6
- adj_mask: int32 [16384, 1024], P('clu'), may hold values 0 or 1
- degrees: int32 [16384], P('clu'), may hold values from 12 to 39
- halo_rows: int32 [16, 16, 32], P('clu'), may hold values from 0 to 1023
- halo_dest: int32 [16, 16, 32], P('clu'), may hold values from 0 to 1023
- halo_count: int32 [16, 16], P('clu'), may hold values from 0 to 32, as said below
- w_first: bfloat16 [2048, 2048], P(None, 'col'), may hold values from -0.75 to 0.75
- b_first: bfloat16 [2048], P('col'), may hold values from -3 to 3
- w_second: bfloat16 [2048, 2048], P(None, 'col'), may hold values from -0.75 to 0.75
- b_second: bfloat16 [2048], P('col'), may hold values from -3 to 3
- out_grad: bfloat16 [16384, 2048], P('clu', 'col'), may hold values from -6 to 6
Outputs:
- first_out: bfloat16 [16384, 2048], P('clu', 'col')
- second_out: bfloat16 [16384, 2048], P('clu', 'col')
- input_grad: float32 [16384, 2048], P('clu', 'col')
- wgrad_first: float32 [2048, 2048], P(None, 'col')
- bgrad_first: float32 [2048], P('col')
- wgrad_second: float32 [2048, 2048], P(None, 'col')
- bgrad_second: float32 [2048], P('col')
Inputs may be any that keep to these rules, and one draw needn't show every extreme that they name: `halo_count`: entry [c, p] counts the used slots, the first ones, from cluster p to cluster c; a cluster sends nothing to itself; every cluster receives 32 from some other cluster.
All inputs are finite; a program needn't handle non-finite values. No bound on the sum of `adj_mask` on one device may be relied on, other than what follows from the above.
Results may differ from a plain program's by a relative error of at most 0.011.
Values may be sent and summed in bfloat16 or wider, within the bound.
A program may use at most 192 MiB of HBM per device.

v0:
```python
import jax
import jax.numpy as jnp
from jax import lax
from jax.sharding import PartitionSpec as P


def activate(pre_act):
    return jax.nn.gelu(pre_act, approximate=True)


def shards(
    features,
    adj_mask,
    degrees,
    halo_rows,
    halo_dest,
    halo_count,
    w_first,
    b_first,
    w_second,
    b_second,
    out_grad,
):
    nodes = features.shape[0]
    peers = halo_rows.shape[1]
    slots = halo_rows.shape[2]
    scale = (1.0 / (degrees.astype(jnp.float32) + 1.0))[:, None]
    adjacency = adj_mask.astype(jnp.bfloat16)
    node_ids = jnp.arange(nodes)[:, None]
    live = (jnp.arange(slots)[None, :] < halo_count[0][:, None]).reshape(-1)
    targets = halo_dest[0].reshape(-1)
    incidence = ((targets[None, :] == node_ids) & live[None, :]).astype(jnp.bfloat16)
    sources = halo_rows[0].reshape(-1)
    source_incidence = (sources[None, :] == node_ids).astype(jnp.bfloat16)
    first_dims = (((0,), (0,)), ((), ()))

    def aggregate(values):
        width = values.shape[1]
        outgoing = jnp.take(values, sources, axis=0).reshape(peers, slots, width)
        incoming = lax.all_to_all(outgoing, "clu", split_axis=0, concat_axis=0, tiled=True)
        inner = jnp.dot(adjacency, values, preferred_element_type=jnp.float32)
        inner = inner + jnp.dot(
            incidence, incoming.reshape(peers * slots, width), preferred_element_type=jnp.float32
        )
        inner = inner + 2.0 * values.astype(jnp.float32)
        return (scale * inner).astype(jnp.bfloat16)

    def forward(values, weight, bias):
        whole = lax.all_gather(values, "col", axis=1, tiled=True)
        mixed = aggregate(whole)
        pre_act = jnp.dot(mixed, weight, preferred_element_type=jnp.float32) + bias.astype(
            jnp.float32
        )
        return (mixed, pre_act)

    def backward(grad_out, mixed, pre_act, weight):
        unused, pull_act = jax.vjp(activate, pre_act)
        grad_pre = pull_act(grad_out.astype(jnp.float32))[0].astype(jnp.bfloat16)
        grad_weight = lax.dot_general(
            mixed, grad_pre, first_dims, preferred_element_type=jnp.float32
        )
        grad_bias = jnp.sum(grad_pre.astype(jnp.float32), axis=0)
        col_terms = lax.dot_general(
            grad_pre, weight, (((1,), (1,)), ((), ())), preferred_element_type=jnp.float32
        )
        grad_mixed = lax.psum_scatter(col_terms, "col", scatter_dimension=1, tiled=True)
        scaled = (scale * grad_mixed).astype(jnp.bfloat16)
        width = scaled.shape[1]
        halo_grad = lax.dot_general(
            incidence, scaled, first_dims, preferred_element_type=jnp.float32
        ).astype(jnp.bfloat16)
        returned = lax.all_to_all(
            halo_grad.reshape(peers, slots, width), "clu", split_axis=0, concat_axis=0, tiled=True
        )
        grad_in = lax.dot_general(adjacency, scaled, first_dims, preferred_element_type=jnp.float32)
        grad_in = grad_in + 2.0 * scaled.astype(jnp.float32)
        grad_in = grad_in + jnp.dot(
            source_incidence,
            returned.reshape(peers * slots, width),
            preferred_element_type=jnp.float32,
        )
        return (grad_in, grad_weight, grad_bias)

    mixed_one, pre_one = forward(features, w_first, b_first)
    first_out = activate(pre_one).astype(jnp.bfloat16)
    mixed_two, pre_two = forward(first_out, w_second, b_second)
    second_out = activate(pre_two).astype(jnp.bfloat16)
    grad_first, wgrad_second, bgrad_second = backward(out_grad, mixed_two, pre_two, w_second)
    input_grad, wgrad_first, bgrad_first = backward(
        grad_first.astype(jnp.bfloat16), mixed_one, pre_one, w_first
    )
    wgrad_second, bgrad_second, wgrad_first, bgrad_first = lax.psum(
        (wgrad_second, bgrad_second, wgrad_first, bgrad_first), "clu"
    )
    return (first_out, second_out, input_grad, wgrad_first, bgrad_first, wgrad_second, bgrad_second)


def solution(mesh):
    return jax.shard_map(
        shards,
        mesh=mesh,
        in_specs=(
            P("clu", "col"),
            P("clu", None),
            P("clu"),
            P("clu", None, None),
            P("clu", None, None),
            P("clu", None),
            P(None, "col"),
            P("col"),
            P(None, "col"),
            P("col"),
            P("clu", "col"),
        ),
        out_specs=(
            P("clu", "col"),
            P("clu", "col"),
            P("clu", "col"),
            P(None, "col"),
            P("col"),
            P(None, "col"),
            P("col"),
        ),
        check_vma=False,
    )
```

profile of v0, /device:TPU:0, one launch (start us, length us, event | category | flops | bytes accessed | tf_op | source)
XLA Modules:
  0.0 798.9 jit_solution(13288473932755501647)
XLA Ops:
  7.2 0.7 all-gather.3.cloned.1.call-update
  7.9 0.8 reshape_squeeze.3
  8.7 17.2 %all-gather.3.cloned.1.call-done = bf16[1024,2048]{1,0:T(8,128)(2,1)} async-done(((bf16[1024,1024]{1,0:T(8,128)(2,1)}), bf16[1024,2048]{1,0:T(8,128)(2,1)}) %all-gather.3.cloned.1.call-update) | async-done | bytes 4194320 | tf_op jit(solution)/shard_map/all_gather | solution.py:49
  25.9 7.1 gather_fusion
  33.1 1.6 broadcast_select_fusion.1
  34.7 6.8 all-to-all-start
  41.6 0.6 all-gather.5.cloned.1.call-start
  42.2 2.8 convert_element_type.72
  45.2 9.4 %fusion.51 = f32[1024,2048]{1,0:T(8,128)} fusion(bf16[1024,1024]{1,0:T(8,128)(2,1)S(1)} %convert_element_type.72, bf16[1024,2048]{1,0:T(8,128)(2,1)} %all-gather.3.cloned.1.call-done), kind=kOutput, calls=%fused_computation.71 | convolution fusion | flops 4294967296 | bytes 14680064 | tf_op jit(solution)/shard_map/dot_general | solution.py:41
  54.6 30.2 %all-to-all-done = bf16[16,32,2048]{2,1,0:T(8,128)(2,1)} async-done(((bf16[16,32,2048]{2,1,0:T(8,128)(2,1)}), bf16[16,32,2048]{2,1,0:T(8,128)(2,1)}, u32[]{:S(2)}, u32[]{:S(2)}) %all-to-all-start) | async-done | bytes 2097184 | tf_op jit(solution)/shard_map/all_to_all | solution.py:40
  84.8 6.9 multiply_convert_fusion
  91.8 7.2 multiply_convert_fusion.4
  99.0 18.6 %all-gather.5.cloned.1.call-done = bf16[1024,2048]{1,0:T(8,128)(2,1)} async-done(((bf16[1024,1024]{1,0:T(8,128)(2,1)}), bf16[1024,2048]{1,0:T(8,128)(2,1)}) %all-gather.5.cloned.1.call-update) | async-done | bytes 4194320 | tf_op jit(solution)/shard_map/all_gather | solution.py:49
  117.7 7.1 gather_fusion.1
  124.8 1.6 broadcast_select_fusion
  126.4 6.8 all-to-all-start.1
  133.2 0.2 reduce-scatter.3.cloned.1.call-start
  133.4 43.0 %all-to-all-done.1 = bf16[16,32,2048]{2,1,0:T(8,128)(2,1)S(1)} async-done(((bf16[16,32,2048]{2,1,0:T(8,128)(2,1)}), bf16[16,32,2048]{2,1,0:T(8,128)(2,1)S(1)}, u32[]{:S(2)}, u32[]{:S(2)}) %all-to-all-start.1) | async-done | bytes 2097184 | tf_op jit(solution)/shard_map/all_to_all | solution.py:40
  176.4 1.3 copy-done.4
  177.8 4.1 fusion.31
  181.9 6.5 fusion.2
  188.4 11.0 %convert_reduce_fusion = (f32[1024]{0:T(1024)S(1)}, bf16[1024,1024]{1,0:T(8,128)(2,1)S(1)}, bf16[1024,1024]{1,0:T(8,128)(2,1)}) fusion(f32[1024]{0:T(1024)S(1)} %convert_element_type.79, bf16[1024,1024]{1,0:T(8,128)(2,1)S(1)} %copy-done.14, bf16[1024,2048]{1,0:T(8,128)(2,1)} %fusion.2, bf16[2048,1024]{1,0:T(8,128)(2,1)S(1)} %copy-done.11), kind=kOutput, calls=%fused_computation.40 | convolution fusion | flops 4322229248 | bytes 14688256 | tf_op jit(solution)/shard_map/dot_general | solution.py:51
  199.4 1.4 copy-done.17
  200.7 6.8 fusion.52
  207.6 21.2 %reduce-scatter.3.cloned.1.call-done = f32[1024,1024]{1,0:T(8,128)} async-done(((f32[1024,2048]{1,0:T(8,128)}), f32[1024,1024]{1,0:T(8,128)}) %reduce-scatter.3.cloned.1.call-update) | async-done | bytes 4194320 | tf_op jit(solution)/shard_map/reduce_scatter | solution.py:66
  228.8 2.5 multiply_convert_fusion.2
  231.2 1.4 copy-done.5
  232.6 2.3 fusion.34
  234.9 6.9 all-to-all-start.2
  241.8 0.3 reduce-scatter.5.cloned.1.call-start
  242.1 6.0 fusion.53
  248.0 18.4 %all-to-all-done.2 = bf16[16,32,1024]{2,1,0:T(8,128)(2,1)S(1)} async-done(((bf16[16,32,1024]{2,1,0:T(8,128)(2,1)}), bf16[16,32,1024]{2,1,0:T(8,128)(2,1)S(1)}, u32[]{:S(2)}, u32[]{:S(2)}) %all-to-all-start.2) | async-done | bytes 1048608 | tf_op jit(solution)/shard_map/all_to_all | solution.py:72
  266.4 7.1 convert_reduce_fusion.1
  273.6 1.3 copy-done.19
  274.9 6.8 fusion.54
  281.7 0.3 all-reduce.4.cloned.1.call-start
  282.0 1.3 copy-done.18
  283.2 9.8 %fusion.57 = f32[2048,1024]{1,0:T(8,128)} fusion(bf16[1024,2048]{1,0:T(8,128)(2,1)} %fusion.2, bf16[1024,1024]{1,0:T(8,128)(2,1)S(1)} %copy-done.18), kind=kOutput, calls=%fused_computation.77 | convolution fusion | flops 4294967296 | bytes 14680064 | tf_op jit(solution)/shard_map/dot_general | solution.py:59
  293.1 6.8 fusion.56
  299.9 2.5 multiply_convert_fusion.1
  302.4 2.3 fusion.37
  304.7 6.2 all-to-all-start.3
  310.8 71.0 %all-reduce = (f32[1024]{0:T(1024)}, f32[1024]{0:T(1024)}) all-reduce(f32[1024]{0:T(1024)S(1)} %get-tuple-element.17, f32[1024]{0:T(1024)S(1)} %get-tuple-element.12), channel_id=1, replica_groups=mesh['clu'=16,'col'=2] {'clu'}, use_global_device_ids=true, to_apply=%region_4.6 | all-reduce | flops 2048 | bytes 16384 | tf_op jit(solution)/shard_map/psum | solution.py:92
  381.8 6.0 fusion.55
  387.8 5.6 fusion.23
  393.4 386.7 %all-reduce.4.cloned.1.call-done = (f32[2048,1024]{1,0:T(8,128)}, f32[2048,1024]{1,0:T(8,128)}) async-done(((f32[2048,1024]{1,0:T(8,128)}, f32[2048,1024]{1,0:T(8,128)}), (f32[2048,1024]{1,0:T(8,128)}, f32[2048,1024]{1,0:T(8,128)})) %all-reduce.4.cloned.1.call-update) | async-done | bytes 16777232 | tf_op jit(solution)/shard_map/psum | solution.py:92
  780.2 8.6 %copy.24 = f32[2048,1024]{1,0:T(8,128)} copy(f32[2048,1024]{1,0:T(8,128)} %get-tuple-element.22) | data formatting | bytes 16777216
  788.8 3.4 copy.25
  (53 shorter events, 0.5 us)
Async XLA Ops:
  7.2 18.8 %all-gather.3.cloned.1.call-start = ((), (), s32[]{:S(2)}) async-start(), calls=%async_computation.6 | async-start | bytes 6291456 | tf_op jit(solution)/shard_map/all_gather | solution.py:49
  33.1 9.1 %copy-start.8 = (bf16[1024]{0:T(1024)(128)(2,1)S(1)}, bf16[1024]{0:T(1024)(128)(2,1)}, u32[]{:S(2)}) copy-start(bf16[1024]{0:T(1024)(128)(2,1)} %param.20) | copy-start | bytes 6148
  34.7 50.1 %all-to-all-start = ((bf16[16,32,2048]{2,1,0:T(8,128)(2,1)}), bf16[16,32,2048]{2,1,0:T(8,128)(2,1)}, u32[]{:S(2)}, u32[]{:S(2)}) async-start(bf16[16,32,2048]{2,1,0:T(8,128)(2,1)} %bitcast.55), calls=%async_computation | async-start | bytes 4194304 | tf_op jit(solution)/shard_map/all_to_all | solution.py:40
  41.5 3.4 copy-start.6
  41.5 3.5 copy-start.10
  41.5 3.6 copy-start.7
  41.6 76.1 %all-gather.5.cloned.1.call-start = ((), (), s32[]{:S(2)}) async-start(), calls=%async_computation.7 | async-start | bytes 6291456 | tf_op jit(solution)/shard_map/all_gather | solution.py:49
  44.9 9.6 %copy-start.2 = (bf16[1024,1024]{1,0:T(8,128)(2,1)}, bf16[1024,1024]{1,0:T(8,128)(2,1)S(1)}, u32[]{:S(2)}) copy-start(bf16[1024,1024]{1,0:T(8,128)(2,1)S(1)} %convert_element_type.72) | copy-start | bytes 6291460
  84.8 7.0 copy-start.12
  91.8 7.3 copy-start.15
  124.8 8.6 %copy-start.9 = (bf16[1024]{0:T(1024)(128)(2,1)S(1)}, bf16[1024]{0:T(1024)(128)(2,1)}, u32[]{:S(2)}) copy-start(bf16[1024]{0:T(1024)(128)(2,1)} %param.22) | copy-start | bytes 6148
  126.4 50.0 %all-to-all-start.1 = ((bf16[16,32,2048]{2,1,0:T(8,128)(2,1)}), bf16[16,32,2048]{2,1,0:T(8,128)(2,1)S(1)}, u32[]{:S(2)}, u32[]{:S(2)}) async-start(bf16[16,32,2048]{2,1,0:T(8,128)(2,1)} %bitcast.56), calls=%async_computation.1 | async-start | bytes 4194304 | tf_op jit(solution)/shard_map/all_to_all | solution.py:40
  133.2 95.6 %reduce-scatter.3.cloned.1.call-start = ((), (), s32[]{:S(2)}) async-start(), calls=%async_computation.8 | async-start | bytes 12582912 | tf_op jit(solution)/shard_map/reduce_scatter | solution.py:66
  176.4 1.3 copy-start.4
  177.7 4.1 copy-start
  177.8 4.1 copy-start.3
  181.9 6.6 copy-start.11
  181.9 6.6 copy-start.14
  199.4 1.4 copy-start.17
  231.2 1.4 copy-start.5
  234.9 31.5 %all-to-all-start.2 = ((bf16[16,32,1024]{2,1,0:T(8,128)(2,1)}), bf16[16,32,1024]{2,1,0:T(8,128)(2,1)S(1)}, u32[]{:S(2)}, u32[]{:S(2)}) async-start(bf16[16,32,1024]{2,1,0:T(8,128)(2,1)} %bitcast.61), calls=%async_computation.3 | async-start | bytes 2097152 | tf_op jit(solution)/shard_map/all_to_all | solution.py:72
  241.8 58.1 %reduce-scatter.5.cloned.1.call-start = ((), (), s32[]{:S(2)}) async-start(), calls=%async_computation.9 | async-start | bytes 12582912 | tf_op jit(solution)/shard_map/reduce_scatter | solution.py:66
  266.4 8.5 %copy-start.13 = (bf16[2048,1024]{1,0:T(8,128)(2,1)S(1)}, bf16[2048,1024]{1,0:T(8,128)(2,1)}, u32[]{:S(2)}) copy-start(bf16[2048,1024]{1,0:T(8,128)(2,1)} %param.19) | copy-start | bytes 12582916
  273.5 1.3 copy-start.19
  281.6 1.6 copy-start.18
  281.7 498.5 %all-reduce.4.cloned.1.call-start = ((), (), s32[]{:S(2)}) async-start(), calls=%async_computation.10 | async-start | bytes 33554432 | tf_op jit(solution)/shard_map/psum | solution.py:92
  283.2 9.8 %copy-start.16 = (bf16[1024,2048]{1,0:T(8,128)(2,1)S(1)}, bf16[1024,2048]{1,0:T(8,128)(2,1)}, u32[]{:S(2)}) copy-start(bf16[1024,2048]{1,0:T(8,128)(2,1)} %copy-done.15) | copy-start | bytes 12582916
  283.2 9.8 %copy-start.20 = (bf16[1024,1024]{1,0:T(8,128)(2,1)S(1)}, bf16[1024,1024]{1,0:T(8,128)(2,1)}, u32[]{:S(2)}) copy-start(bf16[1024,1024]{1,0:T(8,128)(2,1)} %copy-done.19) | copy-start | bytes 6291460
  304.7 83.1 %all-to-all-start.3 = ((bf16[16,32,1024]{2,1,0:T(8,128)(2,1)}), bf16[16,32,1024]{2,1,0:T(8,128)(2,1)S(1)}, u32[]{:S(2)}, u32[]{:S(2)}) async-start(bf16[16,32,1024]{2,1,0:T(8,128)(2,1)} %bitcast.60), calls=%async_computation.5 | async-start | bytes 2097152 | tf_op jit(solution)/shard_map/all_to_all | solution.py:72
  780.2 8.6 %copy-start.1 = (f32[2048,1024]{1,0:T(8,128)S(1)}, f32[2048,1024]{1,0:T(8,128)}, u32[]{:S(2)}) copy-start(f32[2048,1024]{1,0:T(8,128)} %get-tuple-element.24) | copy-start | bytes 25165828
Sparse Core Ops, SparseCore 0:
  9.5 16.3 all-gather.2
  99.2 18.4 all-gather.4
  207.7 21.0 reduce-scatter.2
  281.8 16.8 reduce-scatter.4
  305.6 474.5 all-reduce.3
where the time goes:
time: 803 us; the launch traced here: 799 us
  waiting for transfers between devices  536 us (67%)
  matrix products  105 us (13%)
  blocking collectives  71 us (9%)
  local copies, waits for them, and re-layouts  33.9 us (4%)
  starting transfers between devices  28 us (3%)
  between operations  14.3 us (2%)
  other arithmetic  11 us (1%)
    psum x1, waiting for transfers between devices, shards(): lax.psum((wgrad_second, bgrad_second, wgrad_first, bgrad_first), 'clu')  387 us
    all_to_all x2, waiting for transfers between devices, aggregate(): lax.all_to_all(outgoing, 'clu', split_axis=0, concat_axis=0, tiled=True)  73.2 us
    psum x1, blocking collectives, shards(): lax.psum((wgrad_second, bgrad_second, wgrad_first, bgrad_first), 'clu')  71 us
    all_gather x2, waiting for transfers between devices, forward(): whole = lax.all_gather(values, 'col', axis=1, tiled=True)  35.9 us
    reduce_scatter x2, waiting for transfers between devices, backward(): lax.psum_scatter(col_terms, 'col', scatter_dimension=1, tiled=True)  21.2 us
    unnamed x44, local copies, waits for them, and re-layouts  18.7 us
    all_to_all x2, waiting for transfers between devices, backward(): lax.all_to_all(halo_grad.reshape(peers, slots, width), 'clu', split_axis=...  18.4 us
    dot_general x2, matrix products, forward(): jnp.dot(mixed, weight, preferred_element_type=jnp.float32)  18.2 us
  transfers between devices with their start and end apart: 9, of which 7 were waited for; matrix products, arithmetic and copies ran while one was open for 7% of the time, Pallas kernels for 0%

commit v1 on v0

v1 whole, which is shorter than its diff:
```python
import jax
import jax.numpy as jnp
from jax import lax
from jax.sharding import PartitionSpec as P

F32 = jnp.float32
BF16 = jnp.bfloat16


def activate(pre_act):
    return jax.nn.gelu(pre_act, approximate=True)


def dot(a, b, dims):
    return lax.dot_general(a, b, (dims, ((), ())), preferred_element_type=F32)


ROWS_COLS = ((1,), (0,))
TRANSPOSED = ((0,), (0,))
BY_ROWS = ((1,), (1,))


def flip(x, bit, members):
    return lax.ppermute(x, "clu", [(i, i ^ (1 << bit)) for i in range(members)])


def total_rows(part, order, members):
    index = lax.axis_index("clu")
    for bit in order:
        half = part.shape[0] // 2
        mine = (index >> bit) & 1
        keep = lax.dynamic_slice_in_dim(part, mine * half, half, 0)
        give = lax.dynamic_slice_in_dim(part, (1 - mine) * half, half, 0)
        got = flip(give, bit, members)
        part = (keep.astype(F32) + got.astype(F32)).astype(BF16)
    for bit in reversed(order):
        mine = (index >> bit) & 1
        got = flip(part, bit, members)
        part = jnp.where(
            mine == 0, jnp.concatenate([part, got]), jnp.concatenate([got, part])
        )
    return part


def total_small(x, bits, members):
    for bit in range(bits):
        x = x + flip(x, bit, members)
    return x


def shards(
    features,
    adj_mask,
    degrees,
    halo_rows,
    halo_dest,
    halo_count,
    w_first,
    b_first,
    w_second,
    b_second,
    out_grad,
):
    nodes, width = features.shape
    peers = halo_rows.shape[1]
    slots = halo_rows.shape[2]
    bits = peers.bit_length() - 1
    col = lax.axis_index("col")
    scale = (1.0 / (degrees.astype(F32) + 1.0))[:, None]
    node_ids = jnp.arange(nodes)
    adjacency = (adj_mask + 2 * (node_ids[:, None] == node_ids[None, :])).astype(BF16)
    live = (jnp.arange(slots)[None, :] < halo_count[0][:, None]).reshape(-1)
    targets = halo_dest[0].reshape(-1)
    incidence = ((targets[None, :] == node_ids[:, None]) & live[None, :]).astype(BF16)
    sources = halo_rows[0].reshape(-1)
    pick = (sources[:, None] == node_ids[None, :]).astype(BF16)

    def swap(x):
        return lax.ppermute(x, "col", [(0, 1), (1, 0)])

    def exchange(rows):
        out = lax.all_to_all(
            rows.reshape(peers, slots, width), "clu", split_axis=0, concat_axis=0, tiled=True
        )
        return out.reshape(peers * slots, width)

    def halves(weight):
        own = lax.dynamic_slice_in_dim(weight, col * width, width, 0)
        other = lax.dynamic_slice_in_dim(weight, (1 - col) * width, width, 0)
        return own, other

    def forward(values, weights, bias):
        incoming = exchange(dot(pick, values, ROWS_COLS).astype(BF16))
        inner = dot(adjacency, values, ROWS_COLS) + dot(incidence, incoming, ROWS_COLS)
        mixed = (scale * inner).astype(BF16)
        other = swap(mixed)
        pre_act = dot(mixed, weights[0], ROWS_COLS) + dot(other, weights[1], ROWS_COLS)
        return (mixed, other), pre_act + bias.astype(F32)

    def weight_sum(mixed, grad_pre):
        terms = [dot(m, grad_pre, TRANSPOSED).astype(BF16) for m in mixed]
        cut = nodes_cut(terms[0].shape[0])
        orders = bit_orders(bits)
        own = jnp.concatenate(
            [
                total_rows(terms[0][:cut], orders[0], peers),
                total_rows(terms[0][cut:], orders[2], peers),
            ]
        )
        other = jnp.concatenate(
            [
                total_rows(terms[1][:cut], orders[1], peers),
                total_rows(terms[1][cut:], orders[3], peers),
            ]
        )
        first = jnp.where(col == 0, own, other)
        second = jnp.where(col == 0, other, own)
        return jnp.concatenate([first, second]).astype(F32)

    def backward(grad_out, mixed, pre_act, weights):
        unused, pull_act = jax.vjp(activate, pre_act)
        grad_pre = pull_act(grad_out.astype(F32))[0].astype(BF16)
        grad_weight = weight_sum(mixed, grad_pre)
        grad_bias = total_small(jnp.sum(grad_pre.astype(F32), axis=0), bits, peers)
        sent = swap(dot(grad_pre, weights[1], BY_ROWS).astype(BF16))
        grad_mixed = dot(grad_pre, weights[0], BY_ROWS) + sent.astype(F32)
        scaled = (scale * grad_mixed).astype(BF16)
        returned = exchange(dot(incidence, scaled, TRANSPOSED).astype(BF16))
        grad_in = dot(adjacency, scaled, TRANSPOSED) + dot(pick, returned, TRANSPOSED)
        return grad_in, grad_weight, grad_bias

    weights_one = halves(w_first)
    weights_two = halves(w_second)
    mixed_one, pre_one = forward(features, weights_one, b_first)
    first_out = activate(pre_one).astype(BF16)
    mixed_two, pre_two = forward(first_out, weights_two, b_second)
    second_out = activate(pre_two).astype(BF16)
    grad_first, wgrad_second, bgrad_second = backward(out_grad, mixed_two, pre_two, weights_two)
    input_grad, wgrad_first, bgrad_first = backward(
        grad_first.astype(BF16), mixed_one, pre_one, weights_one
    )
    return (first_out, second_out, input_grad, wgrad_first, bgrad_first, wgrad_second, bgrad_second)


def nodes_cut(rows):
    return rows * 3 // 4


def bit_orders(bits):
    up = list(range(bits))
    x_first = up
    y_first = up[1::-1] + up[2:]
    z_first = up[2:] + up[:2]
    z_then_y = up[2:] + up[1::-1]
    return x_first, y_first, z_first, z_then_y


def solution(mesh):
    return jax.shard_map(
        shards,
        mesh=mesh,
        in_specs=(
            P("clu", "col"),
            P("clu", None),
            P("clu"),
            P("clu", None, None),
            P("clu", None, None),
            P("clu", None),
            P(None, "col"),
            P("col"),
            P(None, "col"),
            P("col"),
            P("clu", "col"),
        ),
        out_specs=(
            P("clu", "col"),
            P("clu", "col"),
            P("clu", "col"),
            P(None, "col"),
            P("col"),
            P(None, "col"),
            P("col"),
        ),
        check_vma=False,
    )
```

time: 803 us -> 459 us (0.57)
  waiting for transfers between devices: 536 us -> 191 us
  starting transfers between devices: 28 us -> 124 us
  blocking collectives: 71 us -> 0 us
  local copies, waits for them, and re-layouts: 33.9 us -> 4.61 us
  other arithmetic: 11 us -> 34.5 us
  between operations: 14.3 us -> 2.35 us
  matrix products: 105 us -> 94.1 us
    psum x1 -> x0, waiting for transfers between devices: 387 us -> none  [shards(): lax.psum((wgrad_second, bgrad_second, wgrad_first, bgrad_first), 'clu')]
    ppermute x0 -> x76, waiting for transfers between devices: none -> 156 us  [the longest x72 156 us: flip(): return lax.ppermute(x, 'clu', [(i, i ^ 1 << bit) for i in range(members)])]
    ppermute x0 -> x76, starting transfers between devices: none -> 101 us  [the longest x72 101 us: flip(): return lax.ppermute(x, 'clu', [(i, i ^ 1 << bit) for i in range(members)])]
    psum x1 -> x0, blocking collectives: 71 us -> none  [shards(): lax.psum((wgrad_second, bgrad_second, wgrad_first, bgrad_first), 'clu')]
    all_to_all x4, waiting for transfers between devices: 91.6 us -> 34.5 us  [exchange(): lax.all_to_all(rows.reshape(peers, slots, width), 'clu', split_axis=0, co...]
    all_gather x2 -> x0, waiting for transfers between devices: 35.9 us -> none  [forward(): whole = lax.all_gather(values, 'col', axis=1, tiled=True)]
    reduce_scatter x2 -> x0, waiting for transfers between devices: 21.2 us -> none  [backward(): lax.psum_scatter(col_terms, 'col', scatter_dimension=1, tiled=True)]
    select_n x3 -> x34, other arithmetic: 3.16 us -> 20.8 us  [the longest x32 18.2 us: total_rows(): jnp.where(mine == 0, jnp.concatenate([part, got]), jnp.concatenate([got,...]
  transfers between devices with their start and end apart: 9 -> 80, of which waited for: 7 -> 41; matrix products, arithmetic and copies ran while one was open for 7% -> 15% of each run, Pallas kernels for 0% -> 0%
where the time goes in v1:
time: 459 us; the launch traced here: 451 us
  waiting for transfers between devices  191 us (42%)
  starting transfers between devices  124 us (27%)
  matrix products  94.1 us (21%)
  other arithmetic  34.5 us (8%)
  local copies, waits for them, and re-layouts  4.61 us (1%)
    ppermute x72, waiting for transfers between devices, flip(): return lax.ppermute(x, 'clu', [(i, i ^ 1 << bit) for i in range(members)])  156 us
    ppermute x72, starting transfers between devices, flip(): return lax.ppermute(x, 'clu', [(i, i ^ 1 << bit) for i in range(members)])  101 us
    dot_general x24, matrix products, dot(): return lax.dot_general(a, b, (dims, ((), ())), preferred_element_type=F32)  94.1 us
    all_to_all x4, waiting for transfers between devices, exchange(): lax.all_to_all(rows.reshape(peers, slots, width), 'clu', split_axis=0, co...  34.5 us
    all_to_all x4, starting transfers between devices, exchange(): lax.all_to_all(rows.reshape(peers, slots, width), 'clu', split_axis=0, co...  23.7 us
    select_n x32, other arithmetic, total_rows(): jnp.where(mine == 0, jnp.concatenate([part, got]), jnp.concatenate([got,...  18.2 us
  transfers between devices with their start and end apart: 80, of which 41 were waited for; matrix products, arithmetic and copies ran while one was open for 15% of the time, Pallas kernels for 0%

profile of v1, /device:TPU:0, one launch (start us, length us, event | category | flops | bytes accessed | tf_op | source)
XLA Modules:
  0.0 450.7 jit_solution(955767067761716124)
XLA Ops:
  4.5 8.5 %all-to-all-start = ((bf16[16,32,1024]{2,1,0:T(8,128)(2,1)}), bf16[16,32,1024]{2,1,0:T(8,128)(2,1)S(1)}, u32[]{:S(2)}, u32[]{:S(2)}) async-start(bf16[16,32,1024]{2,1,0:T(8,128)(2,1)} %bitcast.43), calls=%async_computation | async-start | bytes 2097152 | tf_op jit(solution)/shard_map/all_to_all | solution.py:82
  13.3 2.8 add_convert_fusion.1
  17.4 4.3 fusion.76
  21.7 15.7 %all-to-all-done = bf16[16,32,1024]{2,1,0:T(8,128)(2,1)S(1)} async-done(((bf16[16,32,1024]{2,1,0:T(8,128)(2,1)}), bf16[16,32,1024]{2,1,0:T(8,128)(2,1)S(1)}, u32[]{:S(2)}, u32[]{:S(2)}) %all-to-all-start) | async-done | bytes 1048608 | tf_op jit(solution)/shard_map/all_to_all | solution.py:82
  37.4 4.8 %multiply_convert_fusion.5 = bf16[1024,1024]{1,0:T(8,128)(2,1)} fusion(f32[1024,1024]{1,0:T(8,128)} %fusion.76, bf16[512,1024]{1,0:T(8,128)(2,1)S(1)} %bitcast.42, f32[1024]{0:T(1024)S(1)} %add_divide_fusion, s32[512]{0:T(512)S(1)} %eq.35, pred[512]{0:T(512)(128)(4,1)S(1)} %lt.71), kind=kOutput, calls=%fused_computation.40 | convolution fusion | flops 1077936128 | bytes 7346688 | tf_op jit(solution)/shard_map/dot_general | solution.py:15
  42.2 4.7 %fusion.41 = f32[1024,1024]{1,0:T(8,128)S(1)} fusion(bf16[1024,1024]{1,0:T(8,128)(2,1)} %multiply_convert_fusion.5, bf16[2048,1024]{1,0:T(8,128)(2,1)} %param.17, s32[]{:T(128)S(6)} %select_n.308), kind=kOutput, calls=%fused_computation.77 | convolution fusion | flops 2147483648 | bytes 8388612 | tf_op jit(solution)/shard_map/dot_general | solution.py:15
  47.0 5.3 %multiply_convert_fusion.4 = (bf16[1024,1024]{1,0:T(8,128)(2,1)S(1)}, f32[1024,1024]{1,0:T(8,128)}) fusion(f32[1024]{0:T(1024)S(1)} %convert_element_type.388, f32[1024,1024]{1,0:T(8,128)S(1)} %fusion.41, bf16[1024,1024]{1,0:T(8,128)(2,1)S(1)} %collective-permute-done, bf16[2048,1024]{1,0:T(8,128)(2,1)S(1)} %copy-done.19, s32[]{:T(128)S(6)} %select_n.309), kind=kOutput, calls=%fused_computation.38 | convolution fusion | flops 2159017984 | bytes 14684164 | tf_op jit(solution)/shard_map/dot_general | solution.py:15
  54.6 6.2 %all-to-all-start.1 = ((bf16[16,32,1024]{2,1,0:T(8,128)(2,1)}), bf16[16,32,1024]{2,1,0:T(8,128)(2,1)S(1)}, u32[]{:S(2)}, u32[]{:S(2)}) async-start(bf16[16,32,1024]{2,1,0:T(8,128)(2,1)} %bitcast.45), calls=%async_computation.1 | async-start | bytes 2097152 | tf_op jit(solution)/shard_map/all_to_all | solution.py:82
  60.8 5.9 %fusion.77 = f32[1024,1024]{1,0:T(8,128)} fusion(bf16[1024,1024]{1,0:T(8,128)(2,1)S(1)} %copy-done.4, bf16[1024,1024]{1,0:T(8,128)(2,1)} %copy-done.24), kind=kOutput, calls=%fused_computation.202 | convolution fusion | flops 2147483648 | bytes 8388608 | tf_op jit(solution)/shard_map/dot_general | solution.py:15
  66.8 18.9 %all-to-all-done.1 = bf16[16,32,1024]{2,1,0:T(8,128)(2,1)S(1)} async-done(((bf16[16,32,1024]{2,1,0:T(8,128)(2,1)}), bf16[16,32,1024]{2,1,0:T(8,128)(2,1)S(1)}, u32[]{:S(2)}, u32[]{:S(2)}) %all-to-all-start.1) | async-done | bytes 1048608 | tf_op jit(solution)/shard_map/all_to_all | solution.py:82
  85.6 4.8 %multiply_convert_fusion.3 = bf16[1024,1024]{1,0:T(8,128)(2,1)} fusion(f32[1024,1024]{1,0:T(8,128)} %fusion.77, bf16[512,1024]{1,0:T(8,128)(2,1)S(1)} %bitcast.44, f32[1024]{0:T(1024)S(1)} %add_divide_fusion, s32[512]{0:T(512)S(1)} %eq.35, pred[512]{0:T(512)(128)(4,1)S(1)} %lt.71), kind=kOutput, calls=%fused_computation.37 | convolution fusion | flops 1077936128 | bytes 7346688 | tf_op jit(solution)/shard_map/dot_general | solution.py:15
  90.5 4.7 %fusion.35 = f32[1024,1024]{1,0:T(8,128)S(1)} fusion(bf16[1024,1024]{1,0:T(8,128)(2,1)} %multiply_convert_fusion.3, bf16[2048,1024]{1,0:T(8,128)(2,1)} %param.19, s32[]{:T(128)S(6)} %select_n.308), kind=kOutput, calls=%fused_computation.71 | convolution fusion | flops 2147483648 | bytes 8388612 | tf_op jit(solution)/shard_map/dot_general | solution.py:15
  95.2 8.7 %convert_reduce_fusion = (f32[1024]{0:T(1024)S(1)}, bf16[1024,1024]{1,0:T(8,128)(2,1)S(1)}, bf16[1024,1024]{1,0:T(8,128)(2,1)}) fusion(bf16[1024,1024]{1,0:T(8,128)(2,1)S(1)} %copy-done.21, f32[1024]{0:T(1024)S(1)} %convert_element_type.392, f32[1024,1024]{1,0:T(8,128)S(1)} %fusion.35, bf16[1024,1024]{1,0:T(8,128)(2,1)} %collective-permute-done.1, ...), kind=kOutput, calls=%fused_computation.30 | convolution fusion | flops 2175794176 | bytes 14688260 | tf_op jit(solution)/shard_map/dot_general | solution.py:15
  104.0 4.0 convolution_convert_fusion.1
  108.2 4.0 convolution_convert_fusion
  112.4 3.4 collective-permute-start.48
  125.1 6.0 %collective-permute-done.64 = bf16[128,1024]{1,0:T(8,128)(2,1)S(1)} collective-permute-done((bf16[128,1024]{1,0:T(8,128)(2,1)S(1)}, bf16[128,1024]{1,0:T(8,128)(2,1)S(1)}, u32[]{:S(2)}, u32[]{:S(2)}) %collective-permute-start.64) | collective-permute-done | bytes 262176 | tf_op jit(solution)/shard_map/ppermute | solution.py:24
  132.4 7.1 %collective-permute-done.65 = bf16[64,1024]{1,0:T(8,128)(2,1)S(1)} collective-permute-done((bf16[64,1024]{1,0:T(8,128)(2,1)S(1)}, bf16[64,1024]{1,0:T(8,128)(2,1)S(1)}, u32[]{:S(2)}, u32[]{:S(2)}) %collective-permute-start.65) | collective-permute-done | bytes 131104 | tf_op jit(solution)/shard_map/ppermute | solution.py:24
  150.6 6.4 %collective-permute-done.41 = bf16[192,1024]{1,0:T(8,128)(2,1)S(1)} collective-permute-done((bf16[192,1024]{1,0:T(8,128)(2,1)S(1)}, bf16[192,1024]{1,0:T(8,128)(2,1)S(1)}, u32[]{:S(2)}, u32[]{:S(2)}) %collective-permute-start.41) | collective-permute-done | bytes 393248 | tf_op jit(solution)/shard_map/ppermute | solution.py:24
  159.5 5.2 %collective-permute-done.42 = bf16[96,1024]{1,0:T(8,128)(2,1)S(1)} collective-permute-done((bf16[96,1024]{1,0:T(8,128)(2,1)S(1)}, bf16[96,1024]{1,0:T(8,128)(2,1)S(1)}, u32[]{:S(2)}, u32[]{:S(2)}) %collective-permute-start.42) | collective-permute-done | bytes 196640 | tf_op jit(solution)/shard_map/ppermute | solution.py:24
  168.1 7.0 %collective-permute-done.43 = bf16[48,1024]{1,0:T(8,128)(2,1)S(1)} collective-permute-done((bf16[48,1024]{1,0:T(8,128)(2,1)S(1)}, bf16[48,1024]{1,0:T(8,128)(2,1)S(1)}, u32[]{:S(2)}, u32[]{:S(2)}) %collective-permute-start.43) | collective-permute-done | bytes 98336 | tf_op jit(solution)/shard_map/ppermute | solution.py:24
  178.2 3.6 collective-permute-done.44
  186.8 4.3 all-to-all-start.2
  196.3 11.8 %collective-permute-done.61 = bf16[96,1024]{1,0:T(8,128)(2,1)S(1)} collective-permute-done((bf16[96,1024]{1,0:T(8,128)(2,1)S(1)}, bf16[96,1024]{1,0:T(8,128)(2,1)S(1)}, u32[]{:S(2)}, u32[]{:S(2)}) %collective-permute-start.61) | collective-permute-done | bytes 196640 | tf_op jit(solution)/shard_map/ppermute | solution.py:24
  211.7 6.5 %collective-permute-start.54 = (bf16[64,1024]{1,0:T(8,128)(2,1)S(1)}, bf16[64,1024]{1,0:T(8,128)(2,1)S(1)}, u32[]{:S(2)}, u32[]{:S(2)}) collective-permute-start(bf16[64,1024]{1,0:T(8,128)(2,1)S(1)} %maximum_select_fusion.26), channel_id=1, source_target_pairs={{0,16},{2,18},{4,20},{6,22},{8,24},{10,26},{12,28},{14,30},{16,0},... | collective-permute-start | bytes 393224 | tf_op jit(solution)/shard_map/ppermute | solution.py:24
  228.1 5.7 %collective-permute-done.72 = f32[1024]{0:T(1024)S(1)} collective-permute-done((f32[1024]{0:T(1024)S(1)}, f32[1024]{0:T(1024)S(1)}, u32[]{:S(2)}, u32[]{:S(2)}) %collective-permute-start.72) | collective-permute-done | bytes 4128 | tf_op jit(solution)/shard_map/ppermute | solution.py:24
  234.4 2.9 collective-permute-done.73
  240.9 3.1 collective-permute-start.75
  255.8 6.9 %convert_reduce_fusion.1 = (f32[1024]{0:T(1024)S(1)}, bf16[1024,1024]{1,0:T(8,128)(2,1)S(1)}) fusion(f32[1024,1024]{1,0:T(8,128)} %get-tuple-element.15, f32[1024,1024]{1,0:T(8,128)S(1)} %fusion.21, bf16[1024,1024]{1,0:T(8,128)(2,1)S(1)} %copy-done.5, bf16[1024,1024]{1,0:T(8,128)(2,1)S(1)} %copy-done.28), kind=kOutput, calls=%fused_computation.31 | convolution fusion | flops 2173697024 | bytes 14684160 | tf_op jit(solution)/shard_map/dot_general | solution.py:15
  262.8 4.1 convolution_convert_fusion.3
  287.2 8.2 %collective-permute-done.13 = bf16[64,1024]{1,0:T(8,128)(2,1)S(1)} collective-permute-done((bf16[64,1024]{1,0:T(8,128)(2,1)S(1)}, bf16[64,1024]{1,0:T(8,128)(2,1)S(1)}, u32[]{:S(2)}, u32[]{:S(2)}) %collective-permute-start.13) | collective-permute-done | bytes 131104 | tf_op jit(solution)/shard_map/ppermute | solution.py:24
  295.4 7.3 %collective-permute-done.29 = bf16[64,1024]{1,0:T(8,128)(2,1)S(1)} collective-permute-done((bf16[64,1024]{1,0:T(8,128)(2,1)S(1)}, bf16[64,1024]{1,0:T(8,128)(2,1)S(1)}, u32[]{:S(2)}, u32[]{:S(2)}) %collective-permute-start.29) | collective-permute-done | bytes 131104 | tf_op jit(solution)/shard_map/ppermute | solution.py:24
  328.7 3.1 collective-permute-done.17
  338.6 3.5 collective-permute-done.5
  342.1 2.9 collective-permute-start.34
  346.0 5.4 %collective-permute-done.6 = bf16[96,1024]{1,0:T(8,128)(2,1)S(1)} collective-permute-done((bf16[96,1024]{1,0:T(8,128)(2,1)S(1)}, bf16[96,1024]{1,0:T(8,128)(2,1)S(1)}, u32[]{:S(2)}, u32[]{:S(2)}) %collective-permute-start.6) | collective-permute-done | bytes 196640 | tf_op jit(solution)/shard_map/ppermute | solution.py:24
  353.4 4.7 %collective-permute-done.22 = bf16[96,1024]{1,0:T(8,128)(2,1)S(1)} collective-permute-done((bf16[96,1024]{1,0:T(8,128)(2,1)S(1)}, bf16[96,1024]{1,0:T(8,128)(2,1)S(1)}, u32[]{:S(2)}, u32[]{:S(2)}) %collective-permute-start.22) | collective-permute-done | bytes 196640 | tf_op jit(solution)/shard_map/ppermute | solution.py:24
  360.0 4.8 %collective-permute-done.7 = bf16[48,1024]{1,0:T(8,128)(2,1)S(1)} collective-permute-done((bf16[48,1024]{1,0:T(8,128)(2,1)S(1)}, bf16[48,1024]{1,0:T(8,128)(2,1)S(1)}, u32[]{:S(2)}, u32[]{:S(2)}) %collective-permute-start.7) | collective-permute-done | bytes 98336 | tf_op jit(solution)/shard_map/ppermute | solution.py:24
  365.5 5.1 %collective-permute-done.23 = bf16[48,1024]{1,0:T(8,128)(2,1)S(1)} collective-permute-done((bf16[48,1024]{1,0:T(8,128)(2,1)S(1)}, bf16[48,1024]{1,0:T(8,128)(2,1)S(1)}, u32[]{:S(2)}, u32[]{:S(2)}) %collective-permute-start.23) | collective-permute-done | bytes 98336 | tf_op jit(solution)/shard_map/ppermute | solution.py:24
  371.4 4.8 %collective-permute-done.8 = bf16[48,1024]{1,0:T(8,128)(2,1)S(1)} collective-permute-done((bf16[48,1024]{1,0:T(8,128)(2,1)S(1)}, bf16[48,1024]{1,0:T(8,128)(2,1)S(1)}, u32[]{:S(2)}, u32[]{:S(2)}) %collective-permute-start.8) | collective-permute-done | bytes 98336 | tf_op jit(solution)/shard_map/ppermute | solution.py:24
  377.7 4.1 collective-permute-done.24
  381.8 2.8 collective-permute-start.9
  395.4 11.3 %collective-permute-done.10 = bf16[192,1024]{1,0:T(8,128)(2,1)S(1)} collective-permute-done((bf16[192,1024]{1,0:T(8,128)(2,1)S(1)}, bf16[192,1024]{1,0:T(8,128)(2,1)S(1)}, u32[]{:S(2)}, u32[]{:S(2)}) %collective-permute-start.10) | collective-permute-done | bytes 393248 | tf_op jit(solution)/shard_map/ppermute | solution.py:24
  411.3 4.7 %all-to-all-start.3 = ((bf16[16,32,1024]{2,1,0:T(8,128)(2,1)}), bf16[16,32,1024]{2,1,0:T(8,128)(2,1)}, u32[]{:S(2)}, u32[]{:S(2)}) async-start(bf16[16,32,1024]{2,1,0:T(8,128)(2,1)} %bitcast.41), calls=%async_computation.3 | async-start | bytes 2097152 | tf_op jit(solution)/shard_map/all_to_all | solution.py:82
  425.6 5.3 %collective-permute-done.35 = bf16[128,1024]{1,0:T(8,128)(2,1)S(1)} collective-permute-done((bf16[128,1024]{1,0:T(8,128)(2,1)S(1)}, bf16[128,1024]{1,0:T(8,128)(2,1)S(1)}, u32[]{:S(2)}, u32[]{:S(2)}) %collective-permute-start.35) | collective-permute-done | bytes 262176 | tf_op jit(solution)/shard_map/ppermute | solution.py:24
  435.9 7.0 %maximum_convert_fusion = (f32[2048,1024]{1,0:T(8,128)}, f32[2048,1024]{1,0:T(8,128)}) fusion(bf16[1024,1024]{1,0:T(8,128)(2,1)S(1)} %get-tuple-element.12, bf16[1024,1024]{1,0:T(8,128)(2,1)S(1)} %get-tuple-element.11, bf16[1024,1024]{1,0:T(8,128)(2,1)S(1)} %get-tuple-element.10, bf16[1024,1024]{1,0:T(8,128)(2,1)S(1)} %get-tuple-element.9), kind=kLoop, calls=%fused_computation.28 | loop fusion | flops 16777216 | bytes 25165824 | tf_op jit(solution)/shard_map/convert_element_type | solution.py:118
  442.9 2.8 fusion.20
  445.7 4.6 %convolution_add_fusion = f32[1024,1024]{1,0:T(8,128)} fusion(f32[1024,1024]{1,0:T(8,128)S(1)} %fusion.20, bf16[1024,1024]{1,0:T(8,128)(2,1)S(1)} %copy-done.6, bf16[1024,1024]{1,0:T(8,128)(2,1)S(1)} %copy-done.26), kind=kOutput, calls=%fused_computation.60 | convolution fusion | flops 2148532224 | bytes 12582912 | tf_op jit(solution)/shard_map/dot_general | solution.py:15
  (317 shorter events, 168.3 us)
Async XLA Ops:
  4.5 32.9 %all-to-all-start = ((bf16[16,32,1024]{2,1,0:T(8,128)(2,1)}), bf16[16,32,1024]{2,1,0:T(8,128)(2,1)S(1)}, u32[]{:S(2)}, u32[]{:S(2)}) async-start(bf16[16,32,1024]{2,1,0:T(8,128)(2,1)} %bitcast.43), calls=%async_computation | async-start | bytes 2097152 | tf_op jit(solution)/shard_map/all_to_all | solution.py:82
  54.6 31.0 %all-to-all-start.1 = ((bf16[16,32,1024]{2,1,0:T(8,128)(2,1)}), bf16[16,32,1024]{2,1,0:T(8,128)(2,1)S(1)}, u32[]{:S(2)}, u32[]{:S(2)}) async-start(bf16[16,32,1024]{2,1,0:T(8,128)(2,1)} %bitcast.45), calls=%async_computation.1 | async-start | bytes 2097152 | tf_op jit(solution)/shard_map/all_to_all | solution.py:82
  112.4 10.5 %collective-permute-start.48 = (bf16[128,1024]{1,0:T(8,128)(2,1)S(1)}, bf16[128,1024]{1,0:T(8,128)(2,1)S(1)}, u32[]{:S(2)}, u32[]{:S(2)}) collective-permute-start(bf16[128,1024]{1,0:T(8,128)(2,1)S(1)} %constant_dynamic-slice_fusion.11), channel_id=1, source_target_pairs={{0,8},{2,10},{4,12},{6,14},{8,0},{10,2},{12,4},{14,6},{16,24},{18,... | collective-permute-start | bytes 786440 | tf_op jit(solution)/shard_map/ppermute | solution.py:24
  115.8 15.4 %collective-permute-start.64 = (bf16[128,1024]{1,0:T(8,128)(2,1)S(1)}, bf16[128,1024]{1,0:T(8,128)(2,1)S(1)}, u32[]{:S(2)}, u32[]{:S(2)}) collective-permute-start(bf16[128,1024]{1,0:T(8,128)(2,1)S(1)} %constant_dynamic-slice_fusion.3), channel_id=1, source_target_pairs={{0,8},{2,10},{4,12},{6,14},{8,0},{10,2},{12,4},{14,6},{16,24},{18,... | collective-permute-start | bytes 786440 | tf_op jit(solution)/shard_map/ppermute | solution.py:24
  115.9 31.0 %collective-permute-start.40 = (bf16[384,1024]{1,0:T(8,128)(2,1)S(1)}, bf16[384,1024]{1,0:T(8,128)(2,1)S(1)}, u32[]{:S(2)}, u32[]{:S(2)}) collective-permute-start(bf16[384,1024]{1,0:T(8,128)(2,1)S(1)} %constant_dynamic-slice_fusion.15), channel_id=1, source_target_pairs={{0,2},{2,0},{4,6},{6,4},{8,10},{10,8},{12,14},{14,12},{16,18},{18,... | collective-permute-start | bytes 2359304 | tf_op jit(solution)/shard_map/ppermute | solution.py:24
  116.8 31.3 %collective-permute-start.56 = (bf16[384,1024]{1,0:T(8,128)(2,1)S(1)}, bf16[384,1024]{1,0:T(8,128)(2,1)S(1)}, u32[]{:S(2)}, u32[]{:S(2)}) collective-permute-start(bf16[384,1024]{1,0:T(8,128)(2,1)S(1)} %constant_dynamic-slice_fusion.7), channel_id=1, source_target_pairs={{0,4},{2,6},{4,0},{6,2},{8,12},{10,14},{12,8},{14,10},{16,20},{18,... | collective-permute-start | bytes 2359304 | tf_op jit(solution)/shard_map/ppermute | solution.py:24
  120.5 61.4 %collective-permute-start.2 = (bf16[1024,1024]{1,0:T(8,128)(2,1)S(1)}, bf16[1024,1024]{1,0:T(8,128)(2,1)S(1)}, u32[]{:S(2)}, u32[]{:S(2)}) collective-permute-start(bf16[1024,1024]{1,0:T(8,128)(2,1)S(1)} %convolution_convert_fusion.5), channel_id=1, source_target_pairs={{0,1},{1,0},{2,3},{3,2},{4,5},{5,4},{6,7},{7,6},{8,9},{9,8},{10,11... | collective-permute-start | bytes 6291464 | tf_op jit(solution)/shard_map/ppermute | solution.py:79
  123.0 8.5 %collective-permute-start.49 = (bf16[64,1024]{1,0:T(8,128)(2,1)S(1)}, bf16[64,1024]{1,0:T(8,128)(2,1)S(1)}, u32[]{:S(2)}, u32[]{:S(2)}) collective-permute-start(bf16[64,1024]{1,0:T(8,128)(2,1)S(1)} %constant_dynamic-slice_fusion.10), channel_id=1, source_target_pairs={{0,16},{2,18},{4,20},{6,22},{8,24},{10,26},{12,28},{14,30},{16,0},... | collective-permute-start | bytes 393224 | tf_op jit(solution)/shard_map/ppermute | solution.py:24
  131.2 8.3 %collective-permute-start.65 = (bf16[64,1024]{1,0:T(8,128)(2,1)S(1)}, bf16[64,1024]{1,0:T(8,128)(2,1)S(1)}, u32[]{:S(2)}, u32[]{:S(2)}) collective-permute-start(bf16[64,1024]{1,0:T(8,128)(2,1)S(1)} %constant_dynamic-slice_fusion.2), channel_id=1, source_target_pairs={{0,16},{2,18},{4,20},{6,22},{8,24},{10,26},{12,28},{14,30},{16,0},... | collective-permute-start | bytes 393224 | tf_op jit(solution)/shard_map/ppermute | solution.py:24
  131.5 10.0 %collective-permute-start.50 = (bf16[32,1024]{1,0:T(8,128)(2,1)S(1)}, bf16[32,1024]{1,0:T(8,128)(2,1)S(1)}, u32[]{:S(2)}, u32[]{:S(2)}) collective-permute-start(bf16[32,1024]{1,0:T(8,128)(2,1)S(1)} %constant_dynamic-slice_fusion.9), channel_id=1, source_target_pairs={{0,2},{2,0},{4,6},{6,4},{8,10},{10,8},{12,14},{14,12},{16,18},{18,... | collective-permute-start | bytes 196616 | tf_op jit(solution)/shard_map/ppermute | solution.py:24
  145.6 49.1 %collective-permute-start.52 = (bf16[16,1024]{1,0:T(8,128)(2,1)S(1)}, bf16[16,1024]{1,0:T(8,128)(2,1)S(1)}, u32[]{:S(2)}, u32[]{:S(2)}) collective-permute-start(bf16[16,1024]{1,0:T(8,128)(2,1)S(1)} %add_convert_fusion.31), channel_id=1, source_target_pairs={{0,4},{2,6},{4,0},{6,2},{8,12},{10,14},{12,8},{14,10},{16,20},{18,... | collective-permute-start | bytes 98312 | tf_op jit(solution)/shard_map/ppermute | solution.py:24
  147.2 9.8 %collective-permute-start.41 = (bf16[192,1024]{1,0:T(8,128)(2,1)S(1)}, bf16[192,1024]{1,0:T(8,128)(2,1)S(1)}, u32[]{:S(2)}, u32[]{:S(2)}) collective-permute-start(bf16[192,1024]{1,0:T(8,128)(2,1)S(1)} %constant_dynamic-slice_fusion.14), channel_id=1, source_target_pairs={{0,4},{2,6},{4,0},{6,2},{8,12},{10,14},{12,8},{14,10},{16,20},{18,... | collective-permute-start | bytes 1179656 | tf_op jit(solution)/shard_map/ppermute | solution.py:24
  148.5 9.5 %collective-permute-start.57 = (bf16[192,1024]{1,0:T(8,128)(2,1)S(1)}, bf16[192,1024]{1,0:T(8,128)(2,1)S(1)}, u32[]{:S(2)}, u32[]{:S(2)}) collective-permute-start(bf16[192,1024]{1,0:T(8,128)(2,1)S(1)} %constant_dynamic-slice_fusion.6), channel_id=1, source_target_pairs={{0,2},{2,0},{4,6},{6,4},{8,10},{10,8},{12,14},{14,12},{16,18},{18,... | collective-permute-start | bytes 1179656 | tf_op jit(solution)/shard_map/ppermute | solution.py:24
  149.3 60.4 %collective-permute-start.68 = (bf16[16,1024]{1,0:T(8,128)(2,1)S(1)}, bf16[16,1024]{1,0:T(8,128)(2,1)S(1)}, u32[]{:S(2)}, u32[]{:S(2)}) collective-permute-start(bf16[16,1024]{1,0:T(8,128)(2,1)S(1)} %add_convert_fusion.30), channel_id=1, source_target_pairs={{0,2},{2,0},{4,6},{6,4},{8,10},{10,8},{12,14},{14,12},{16,18},{18,... | collective-permute-start | bytes 98312 | tf_op jit(solution)/shard_map/ppermute | solution.py:24
  158.1 9.5 %collective-permute-start.58 = (bf16[96,1024]{1,0:T(8,128)(2,1)S(1)}, bf16[96,1024]{1,0:T(8,128)(2,1)S(1)}, u32[]{:S(2)}, u32[]{:S(2)}) collective-permute-start(bf16[96,1024]{1,0:T(8,128)(2,1)S(1)} %constant_dynamic-slice_fusion.5), channel_id=1, source_target_pairs={{0,8},{2,10},{4,12},{6,14},{8,0},{10,2},{12,4},{14,6},{16,24},{18,... | collective-permute-start | bytes 589832 | tf_op jit(solution)/shard_map/ppermute | solution.py:24
  164.9 10.3 %collective-permute-start.43 = (bf16[48,1024]{1,0:T(8,128)(2,1)S(1)}, bf16[48,1024]{1,0:T(8,128)(2,1)S(1)}, u32[]{:S(2)}, u32[]{:S(2)}) collective-permute-start(bf16[48,1024]{1,0:T(8,128)(2,1)S(1)} %constant_dynamic-slice_fusion.12), channel_id=1, source_target_pairs={{0,16},{2,18},{4,20},{6,22},{8,24},{10,26},{12,28},{14,30},{16,0},... | collective-permute-start | bytes 294920 | tf_op jit(solution)/shard_map/ppermute | solution.py:24
  167.7 9.6 %collective-permute-start.59 = (bf16[48,1024]{1,0:T(8,128)(2,1)S(1)}, bf16[48,1024]{1,0:T(8,128)(2,1)S(1)}, u32[]{:S(2)}, u32[]{:S(2)}) collective-permute-start(bf16[48,1024]{1,0:T(8,128)(2,1)S(1)} %constant_dynamic-slice_fusion.4), channel_id=1, source_target_pairs={{0,16},{2,18},{4,20},{6,22},{8,24},{10,26},{12,28},{14,30},{16,0},... | collective-permute-start | bytes 294920 | tf_op jit(solution)/shard_map/ppermute | solution.py:24
  177.3 13.9 %collective-permute-start.60 = (bf16[48,1024]{1,0:T(8,128)(2,1)S(1)}, bf16[48,1024]{1,0:T(8,128)(2,1)S(1)}, u32[]{:S(2)}, u32[]{:S(2)}) collective-permute-start(bf16[48,1024]{1,0:T(8,128)(2,1)S(1)} %add_convert_fusion.22), channel_id=1, source_target_pairs={{0,16},{2,18},{4,20},{6,22},{8,24},{10,26},{12,28},{14,30},{16,0},... | collective-permute-start | bytes 294920 | tf_op jit(solution)/shard_map/ppermute | solution.py:24
  181.9 11.3 %collective-permute-start.45 = (bf16[96,1024]{1,0:T(8,128)(2,1)S(1)}, bf16[96,1024]{1,0:T(8,128)(2,1)S(1)}, u32[]{:S(2)}, u32[]{:S(2)}) collective-permute-start(bf16[96,1024]{1,0:T(8,128)(2,1)S(1)} %maximum_select_fusion.22), channel_id=1, source_target_pairs={{0,8},{2,10},{4,12},{6,14},{8,0},{10,2},{12,4},{14,6},{16,24},{18,... | collective-permute-start | bytes 589832 | tf_op jit(solution)/shard_map/ppermute | solution.py:24
  186.8 66.2 %all-to-all-start.2 = ((bf16[16,32,1024]{2,1,0:T(8,128)(2,1)}), bf16[16,32,1024]{2,1,0:T(8,128)(2,1)}, u32[]{:S(2)}, u32[]{:S(2)}) async-start(bf16[16,32,1024]{2,1,0:T(8,128)(2,1)} %bitcast.5), calls=%async_computation.2 | async-start | bytes 2097152 | tf_op jit(solution)/shard_map/all_to_all | solution.py:82
  191.2 16.8 %collective-permute-start.61 = (bf16[96,1024]{1,0:T(8,128)(2,1)S(1)}, bf16[96,1024]{1,0:T(8,128)(2,1)S(1)}, u32[]{:S(2)}, u32[]{:S(2)}) collective-permute-start(bf16[96,1024]{1,0:T(8,128)(2,1)S(1)} %maximum_select_fusion.23), channel_id=1, source_target_pairs={{0,8},{2,10},{4,12},{6,14},{8,0},{10,2},{12,4},{14,6},{16,24},{18,... | collective-permute-start | bytes 589832 | tf_op jit(solution)/shard_map/ppermute | solution.py:24
  193.3 24.9 %collective-permute-start.46 = (bf16[192,1024]{1,0:T(8,128)(2,1)S(1)}, bf16[192,1024]{1,0:T(8,128)(2,1)S(1)}, u32[]{:S(2)}, u32[]{:S(2)}) collective-permute-start(bf16[192,1024]{1,0:T(8,128)(2,1)S(1)} %maximum_select_fusion.14), channel_id=1, source_target_pairs={{0,4},{2,6},{4,0},{6,2},{8,12},{10,14},{12,8},{14,10},{16,20},{18,... | collective-permute-start | bytes 1179656 | tf_op jit(solution)/shard_map/ppermute | solution.py:24
  194.7 16.9 %collective-permute-start.53 = (bf16[32,1024]{1,0:T(8,128)(2,1)S(1)}, bf16[32,1024]{1,0:T(8,128)(2,1)S(1)}, u32[]{:S(2)}, u32[]{:S(2)}) collective-permute-start(bf16[32,1024]{1,0:T(8,128)(2,1)S(1)} %maximum_select_fusion.30), channel_id=1, source_target_pairs={{0,2},{2,0},{4,6},{6,4},{8,10},{10,8},{12,14},{14,12},{16,18},{18,... | collective-permute-start | bytes 196616 | tf_op jit(solution)/shard_map/ppermute | solution.py:24
  208.2 13.0 %collective-permute-start.62 = (bf16[192,1024]{1,0:T(8,128)(2,1)S(1)}, bf16[192,1024]{1,0:T(8,128)(2,1)S(1)}, u32[]{:S(2)}, u32[]{:S(2)}) collective-permute-start(bf16[192,1024]{1,0:T(8,128)(2,1)S(1)} %maximum_select_fusion.15), channel_id=1, source_target_pairs={{0,2},{2,0},{4,6},{6,4},{8,10},{10,8},{12,14},{14,12},{16,18},{18,... | collective-permute-start | bytes 1179656 | tf_op jit(solution)/shard_map/ppermute | solution.py:24
  209.7 8.9 %collective-permute-start.69 = (bf16[32,1024]{1,0:T(8,128)(2,1)S(1)}, bf16[32,1024]{1,0:T(8,128)(2,1)S(1)}, u32[]{:S(2)}, u32[]{:S(2)}) collective-permute-start(bf16[32,1024]{1,0:T(8,128)(2,1)S(1)} %maximum_select_fusion.31), channel_id=1, source_target_pairs={{0,4},{2,6},{4,0},{6,2},{8,12},{10,14},{12,8},{14,10},{16,20},{18,... | collective-permute-start | bytes 196616 | tf_op jit(solution)/shard_map/ppermute | solution.py:24
  211.7 11.9 %collective-permute-start.54 = (bf16[64,1024]{1,0:T(8,128)(2,1)S(1)}, bf16[64,1024]{1,0:T(8,128)(2,1)S(1)}, u32[]{:S(2)}, u32[]{:S(2)}) collective-permute-start(bf16[64,1024]{1,0:T(8,128)(2,1)S(1)} %maximum_select_fusion.26), channel_id=1, source_target_pairs={{0,16},{2,18},{4,20},{6,22},{8,24},{10,26},{12,28},{14,30},{16,0},... | collective-permute-start | bytes 393224 | tf_op jit(solution)/shard_map/ppermute | solution.py:24
  218.5 29.7 %collective-permute-start.47 = (bf16[384,1024]{1,0:T(8,128)(2,1)S(1)}, bf16[384,1024]{1,0:T(8,128)(2,1)}, u32[]{:S(2)}, u32[]{:S(2)}) collective-permute-start(bf16[384,1024]{1,0:T(8,128)(2,1)S(1)} %maximum_select_fusion.6), channel_id=1, source_target_pairs={{0,2},{2,0},{4,6},{6,4},{8,10},{10,8},{12,14},{14,12},{16,18},{18,... | collective-permute-start | bytes 2359304 | tf_op jit(solution)/shard_map/ppermute | solution.py:24
  221.4 28.8 %collective-permute-start.63 = (bf16[384,1024]{1,0:T(8,128)(2,1)S(1)}, bf16[384,1024]{1,0:T(8,128)(2,1)}, u32[]{:S(2)}, u32[]{:S(2)}) collective-permute-start(bf16[384,1024]{1,0:T(8,128)(2,1)S(1)} %maximum_select_fusion.7), channel_id=1, source_target_pairs={{0,4},{2,6},{4,0},{6,2},{8,12},{10,14},{12,8},{14,10},{16,20},{18,... | collective-permute-start | bytes 2359304 | tf_op jit(solution)/shard_map/ppermute | solution.py:24
  223.6 22.6 %collective-permute-start.55 = (bf16[128,1024]{1,0:T(8,128)(2,1)S(1)}, bf16[128,1024]{1,0:T(8,128)(2,1)S(1)}, u32[]{:S(2)}, u32[]{:S(2)}) collective-permute-start(bf16[128,1024]{1,0:T(8,128)(2,1)S(1)} %maximum_select_fusion.18), channel_id=1, source_target_pairs={{0,8},{2,10},{4,12},{6,14},{8,0},{10,2},{12,4},{14,6},{16,24},{18,... | collective-permute-start | bytes 786440 | tf_op jit(solution)/shard_map/ppermute | solution.py:24
  226.0 21.2 %collective-permute-start.71 = (bf16[128,1024]{1,0:T(8,128)(2,1)S(1)}, bf16[128,1024]{1,0:T(8,128)(2,1)S(1)}, u32[]{:S(2)}, u32[]{:S(2)}) collective-permute-start(bf16[128,1024]{1,0:T(8,128)(2,1)S(1)} %maximum_select_fusion.19), channel_id=1, source_target_pairs={{0,8},{2,10},{4,12},{6,14},{8,0},{10,2},{12,4},{14,6},{16,24},{18,... | collective-permute-start | bytes 786440 | tf_op jit(solution)/shard_map/ppermute | solution.py:24
  273.4 10.5 %collective-permute-start.12 = (bf16[128,1024]{1,0:T(8,128)(2,1)S(1)}, bf16[128,1024]{1,0:T(8,128)(2,1)S(1)}, u32[]{:S(2)}, u32[]{:S(2)}) collective-permute-start(bf16[128,1024]{1,0:T(8,128)(2,1)S(1)} %constant_dynamic-slice_fusion.27), channel_id=1, source_target_pairs={{0,8},{2,10},{4,12},{6,14},{8,0},{10,2},{12,4},{14,6},{16,24},{18,... | collective-permute-start | bytes 786440 | tf_op jit(solution)/shard_map/ppermute | solution.py:24
  275.4 10.6 %collective-permute-start.28 = (bf16[128,1024]{1,0:T(8,128)(2,1)S(1)}, bf16[128,1024]{1,0:T(8,128)(2,1)S(1)}, u32[]{:S(2)}, u32[]{:S(2)}) collective-permute-start(bf16[128,1024]{1,0:T(8,128)(2,1)S(1)} %constant_dynamic-slice_fusion.19), channel_id=1, source_target_pairs={{0,8},{2,10},{4,12},{6,14},{8,0},{10,2},{12,4},{14,6},{16,24},{18,... | collective-permute-start | bytes 786440 | tf_op jit(solution)/shard_map/ppermute | solution.py:24
  281.2 52.6 %collective-permute-start.4 = (bf16[384,1024]{1,0:T(8,128)(2,1)S(1)}, bf16[384,1024]{1,0:T(8,128)(2,1)S(1)}, u32[]{:S(2)}, u32[]{:S(2)}) collective-permute-start(bf16[384,1024]{1,0:T(8,128)(2,1)S(1)} %constant_dynamic-slice_fusion.31), channel_id=1, source_target_pairs={{0,2},{2,0},{4,6},{6,4},{8,10},{10,8},{12,14},{14,12},{16,18},{18,... | collective-permute-start | bytes 2359304 | tf_op jit(solution)/shard_map/ppermute | solution.py:24
  282.7 51.6 %collective-permute-start.20 = (bf16[384,1024]{1,0:T(8,128)(2,1)S(1)}, bf16[384,1024]{1,0:T(8,128)(2,1)S(1)}, u32[]{:S(2)}, u32[]{:S(2)}) collective-permute-start(bf16[384,1024]{1,0:T(8,128)(2,1)S(1)} %constant_dynamic-slice_fusion.23), channel_id=1, source_target_pairs={{0,4},{2,6},{4,0},{6,2},{8,12},{10,14},{12,8},{14,10},{16,20},{18,... | collective-permute-start | bytes 2359304 | tf_op jit(solution)/shard_map/ppermute | solution.py:24
  283.9 107.5 %collective-permute-start.3 = (bf16[1024,1024]{1,0:T(8,128)(2,1)S(1)}, bf16[1024,1024]{1,0:T(8,128)(2,1)S(1)}, u32[]{:S(2)}, u32[]{:S(2)}) collective-permute-start(bf16[1024,1024]{1,0:T(8,128)(2,1)S(1)} %convolution_convert_fusion.4), channel_id=1, source_target_pairs={{0,1},{1,0},{2,3},{3,2},{4,5},{5,4},{6,7},{7,6},{8,9},{9,8},{10,11... | collective-permute-start | bytes 6291464 | tf_op jit(solution)/shard_map/ppermute | solution.py:79
  283.9 139.6 %collective-permute-start.39 = (f32[1024]{0:T(1024)S(1)}, f32[1024]{0:T(1024)S(1)}, u32[]{:S(2)}, u32[]{:S(2)}) collective-permute-start(f32[1024]{0:T(1024)S(1)} %add.366), channel_id=1, source_target_pairs={{0,16},{2,18},{4,20},{6,22},{8,24},{10,26},{12,28},{14,30},{16,0},... | collective-permute-start | bytes 12296 | tf_op jit(solution)/shard_map/ppermute | solution.py:24
  286.0 9.3 %collective-permute-start.13 = (bf16[64,1024]{1,0:T(8,128)(2,1)S(1)}, bf16[64,1024]{1,0:T(8,128)(2,1)S(1)}, u32[]{:S(2)}, u32[]{:S(2)}) collective-permute-start(bf16[64,1024]{1,0:T(8,128)(2,1)S(1)} %constant_dynamic-slice_fusion.26), channel_id=1, source_target_pairs={{0,16},{2,18},{4,20},{6,22},{8,24},{10,26},{12,28},{14,30},{16,0},... | collective-permute-start | bytes 393224 | tf_op jit(solution)/shard_map/ppermute | solution.py:24
  333.8 50.8 %collective-permute-start.18 = (bf16[64,1024]{1,0:T(8,128)(2,1)S(1)}, bf16[64,1024]{1,0:T(8,128)(2,1)S(1)}, u32[]{:S(2)}, u32[]{:S(2)}) collective-permute-start(bf16[64,1024]{1,0:T(8,128)(2,1)S(1)} %maximum_select_fusion.24), channel_id=1, source_target_pairs={{0,16},{2,18},{4,20},{6,22},{8,24},{10,26},{12,28},{14,30},{16,0},... | collective-permute-start | bytes 393224 | tf_op jit(solution)/shard_map/ppermute | solution.py:24
  334.3 7.8 %collective-permute-start.5 = (bf16[192,1024]{1,0:T(8,128)(2,1)S(1)}, bf16[192,1024]{1,0:T(8,128)(2,1)S(1)}, u32[]{:S(2)}, u32[]{:S(2)}) collective-permute-start(bf16[192,1024]{1,0:T(8,128)(2,1)S(1)} %constant_dynamic-slice_fusion.30), channel_id=1, source_target_pairs={{0,4},{2,6},{4,0},{6,2},{8,12},{10,14},{12,8},{14,10},{16,20},{18,... | collective-permute-start | bytes 1179656 | tf_op jit(solution)/shard_map/ppermute | solution.py:24
  336.1 9.0 %collective-permute-start.21 = (bf16[192,1024]{1,0:T(8,128)(2,1)S(1)}, bf16[192,1024]{1,0:T(8,128)(2,1)S(1)}, u32[]{:S(2)}, u32[]{:S(2)}) collective-permute-start(bf16[192,1024]{1,0:T(8,128)(2,1)S(1)} %constant_dynamic-slice_fusion.22), channel_id=1, source_target_pairs={{0,2},{2,0},{4,6},{6,4},{8,10},{10,8},{12,14},{14,12},{16,18},{18,... | collective-permute-start | bytes 1179656 | tf_op jit(solution)/shard_map/ppermute | solution.py:24
  342.1 77.4 %collective-permute-start.34 = (bf16[64,1024]{1,0:T(8,128)(2,1)}, bf16[64,1024]{1,0:T(8,128)(2,1)}, u32[]{:S(2)}, u32[]{:S(2)}) collective-permute-start(bf16[64,1024]{1,0:T(8,128)(2,1)} %maximum_select_fusion.25), channel_id=1, source_target_pairs={{0,16},{2,18},{4,20},{6,22},{8,24},{10,26},{12,28},{14,30},{16,0},... | collective-permute-start | bytes 393224 | tf_op jit(solution)/shard_map/ppermute | solution.py:24
  388.2 35.9 %collective-permute-start.19 = (bf16[128,1024]{1,0:T(8,128)(2,1)}, bf16[128,1024]{1,0:T(8,128)(2,1)}, u32[]{:S(2)}, u32[]{:S(2)}) collective-permute-start(bf16[128,1024]{1,0:T(8,128)(2,1)} %maximum_select_fusion.16), channel_id=1, source_target_pairs={{0,8},{2,10},{4,12},{6,14},{8,0},{10,2},{12,4},{14,6},{16,24},{18,... | collective-permute-start | bytes 786440 | tf_op jit(solution)/shard_map/ppermute | solution.py:24
  390.4 16.4 %collective-permute-start.10 = (bf16[192,1024]{1,0:T(8,128)(2,1)S(1)}, bf16[192,1024]{1,0:T(8,128)(2,1)S(1)}, u32[]{:S(2)}, u32[]{:S(2)}) collective-permute-start(bf16[192,1024]{1,0:T(8,128)(2,1)S(1)} %maximum_select_fusion.12), channel_id=1, source_target_pairs={{0,4},{2,6},{4,0},{6,2},{8,12},{10,14},{12,8},{14,10},{16,20},{18,... | collective-permute-start | bytes 1179656 | tf_op jit(solution)/shard_map/ppermute | solution.py:24
  391.4 24.6 %collective-permute-start.26 = (bf16[192,1024]{1,0:T(8,128)(2,1)S(1)}, bf16[192,1024]{1,0:T(8,128)(2,1)}, u32[]{:S(2)}, u32[]{:S(2)}) collective-permute-start(bf16[192,1024]{1,0:T(8,128)(2,1)S(1)} %maximum_select_fusion.13), channel_id=1, source_target_pairs={{0,2},{2,0},{4,6},{6,4},{8,10},{10,8},{12,14},{14,12},{16,18},{18,... | collective-permute-start | bytes 1179656 | tf_op jit(solution)/shard_map/ppermute | solution.py:24
  407.9 23.1 %collective-permute-start.11 = (bf16[384,1024]{1,0:T(8,128)(2,1)}, bf16[384,1024]{1,0:T(8,128)(2,1)}, u32[]{:S(2)}, u32[]{:S(2)}) collective-permute-start(bf16[384,1024]{1,0:T(8,128)(2,1)} %maximum_select_fusion.4), channel_id=1, source_target_pairs={{0,2},{2,0},{4,6},{6,4},{8,10},{10,8},{12,14},{14,12},{16,18},{18,... | collective-permute-start | bytes 2359304 | tf_op jit(solution)/shard_map/ppermute | solution.py:24
  411.3 31.5 %all-to-all-start.3 = ((bf16[16,32,1024]{2,1,0:T(8,128)(2,1)}), bf16[16,32,1024]{2,1,0:T(8,128)(2,1)}, u32[]{:S(2)}, u32[]{:S(2)}) async-start(bf16[16,32,1024]{2,1,0:T(8,128)(2,1)} %bitcast.41), calls=%async_computation.3 | async-start | bytes 2097152 | tf_op jit(solution)/shard_map/all_to_all | solution.py:82
  417.6 16.3 %collective-permute-start.27 = (bf16[384,1024]{1,0:T(8,128)(2,1)S(1)}, bf16[384,1024]{1,0:T(8,128)(2,1)S(1)}, u32[]{:S(2)}, u32[]{:S(2)}) collective-permute-start(bf16[384,1024]{1,0:T(8,128)(2,1)S(1)} %maximum_select_fusion.5), channel_id=1, source_target_pairs={{0,4},{2,6},{4,0},{6,2},{8,12},{10,14},{12,8},{14,10},{16,20},{18,... | collective-permute-start | bytes 2359304 | tf_op jit(solution)/shard_map/ppermute | solution.py:24
  420.7 10.2 %collective-permute-start.35 = (bf16[128,1024]{1,0:T(8,128)(2,1)S(1)}, bf16[128,1024]{1,0:T(8,128)(2,1)S(1)}, u32[]{:S(2)}, u32[]{:S(2)}) collective-permute-start(bf16[128,1024]{1,0:T(8,128)(2,1)S(1)} %maximum_select_fusion.17), channel_id=1, source_target_pairs={{0,8},{2,10},{4,12},{6,14},{8,0},{10,2},{12,4},{14,6},{16,24},{18,... | collective-permute-start | bytes 786440 | tf_op jit(solution)/shard_map/ppermute | solution.py:24
  (61 other events, 692.2 us)
